TPU v7x, 16 devices: a whole 2x2x2 slice. The times are simulated.
16 devices in a mesh: fsdp: 16 (over z, y, x, core).
Axes of the slice: x: 2, y: 2, z: 2, core: 2. Of those that a mesh axis runs over, the one named last changes fastest.
Arguments:
- hidden: bfloat16 [48, 512, 2048], P('fsdp')
- positions: int32 [48, 512], P('fsdp')
- grad_y: bfloat16 [48, 512, 2048], P('fsdp')
- attn_gain: bfloat16 [2048], P('fsdp')
- w_qkv: bfloat16 [2048, 3072], P('fsdp')
- b_qkv: bfloat16 [3072], P('fsdp')
- w_out: bfloat16 [2048, 2048], P('fsdp')
- mlp_gain: bfloat16 [2048], P('fsdp')
- w_up: bfloat16 [2048, 12288], P('fsdp')
- w_down: bfloat16 [6144, 2048], P('fsdp')
Outputs:
- output 1: bfloat16 [48, 512, 2048], P('fsdp')
- output 2: bfloat16 [48, 512, 2048], P('fsdp')
- output 3: float32 [2048], P('fsdp')
- output 4: float32 [2048, 3072], P('fsdp')
- output 5: float32 [3072], P('fsdp')
- output 6: float32 [2048, 2048], P('fsdp')
- output 7: float32 [2048], P('fsdp')
- output 8: float32 [2048, 12288], P('fsdp')
- output 9: float32 [6144, 2048], P('fsdp')
All inputs are finite; a program needn't handle non-finite values.
Results may differ from a plain program's by a relative error of at most 0.0161494.
Values are sent between devices in bfloat16 or wider.
A program may use at most 1 GiB of HBM per device.

v0:
```python
import jax
import jax.numpy as jnp
from jax import lax
from jax.sharding import PartitionSpec as P

HEAD_DIM = 128
ROPE_BASE = 10000.0
EPS = 1e-5


def norm_scale(rows_in):
    return lax.rsqrt(jnp.mean(rows_in * rows_in, axis=-1, keepdims=True) + EPS)


def rope_tables(positions):
    rot_dim = HEAD_DIM // 2
    inv_freq = 1.0 / (ROPE_BASE ** (jnp.arange(0, rot_dim, 2, dtype=jnp.float32) / rot_dim))
    angles = positions.astype(jnp.float32)[:, :, None, None] * inv_freq
    return jnp.cos(angles), jnp.sin(angles)


def rope_turn(head_vals, cos_t, sin_t):
    rot_dim = HEAD_DIM // 2
    lead_shape = head_vals.shape[:-1]
    rot_pairs = head_vals[..., :rot_dim].reshape(lead_shape + (rot_dim // 2, 2))
    even_part = rot_pairs[..., 0]
    odd_part = rot_pairs[..., 1]
    turned = jnp.stack([even_part * cos_t - odd_part * sin_t, odd_part * cos_t + even_part * sin_t], axis=-1)
    return jnp.concatenate([turned.reshape(lead_shape + (rot_dim,)), head_vals[..., rot_dim:]], axis=-1)


def attend_forward(q_rot, k_rot, values):
    seq_len = q_rot.shape[1]
    token_index = jnp.arange(seq_len)
    causal = token_index[:, None] >= token_index[None, :]
    scores = jnp.einsum('bqkgd,bskd->bkgqs', q_rot, k_rot, preferred_element_type=jnp.float32) * HEAD_DIM ** -0.5
    attn_probs = jax.nn.softmax(jnp.where(causal, scores, -1e30), axis=-1)
    probs_low = attn_probs.astype(jnp.bfloat16)
    context = jnp.einsum('bkgqs,bskd->bqkgd', probs_low, values, preferred_element_type=jnp.float32)
    return context.astype(jnp.bfloat16), attn_probs, probs_low


def attend_backward(q_rot, k_rot, values, attn_probs, probs_low, d_context):
    d_probs = jnp.einsum('bqkgd,bskd->bkgqs', d_context, values, preferred_element_type=jnp.float32)
    d_values = jnp.einsum('bkgqs,bqkgd->bskd', probs_low, d_context, preferred_element_type=jnp.float32)
    d_scores = attn_probs * (d_probs - jnp.sum(attn_probs * d_probs, axis=-1, keepdims=True)) * HEAD_DIM ** -0.5
    d_scores = d_scores.astype(jnp.bfloat16)
    d_query = jnp.einsum('bkgqs,bskd->bqkgd', d_scores, k_rot, preferred_element_type=jnp.float32)
    d_key = jnp.einsum('bkgqs,bqkgd->bskd', d_scores, q_rot, preferred_element_type=jnp.float32)
    return d_query, d_key, d_values


def layer_pass(hidden, positions, grad_y, attn_gain, w_qkv, b_qkv, w_out, mlp_gain, w_up, w_down):
    batch_size, seq_len, model_width = hidden.shape
    q_width = w_out.shape[0]
    kv_width = (w_qkv.shape[1] - q_width) // 2
    kv_heads = kv_width // HEAD_DIM
    group_size = q_width // kv_width
    ff_width = w_down.shape[0]
    cos_t, sin_t = rope_tables(positions)
    hid_wide = hidden.astype(jnp.float32)
    inv_one = norm_scale(hid_wide)
    gain_one = attn_gain.astype(jnp.float32)
    normed = (hid_wide * inv_one * gain_one).astype(jnp.bfloat16)
    qkv_proj = jnp.einsum('bsh,hn->bsn', normed, w_qkv, preferred_element_type=jnp.float32) + b_qkv.astype(jnp.float32)
    q_rot = rope_turn(qkv_proj[..., :q_width].reshape(batch_size, seq_len, q_width // HEAD_DIM, HEAD_DIM), cos_t, sin_t)
    q_rot = q_rot.astype(jnp.bfloat16).reshape(batch_size, seq_len, kv_heads, group_size, HEAD_DIM)
    k_rot = rope_turn(qkv_proj[..., q_width:q_width + kv_width].reshape(batch_size, seq_len, kv_heads, HEAD_DIM), cos_t, sin_t).astype(jnp.bfloat16)
    values = qkv_proj[..., q_width + kv_width:].reshape(batch_size, seq_len, kv_heads, HEAD_DIM).astype(jnp.bfloat16)
    context, attn_probs, probs_low = attend_forward(q_rot, k_rot, values)
    context = context.reshape(batch_size, seq_len, q_width)
    mid_state = (hid_wide + jnp.einsum('bsn,nh->bsh', context, w_out, preferred_element_type=jnp.float32)).astype(jnp.bfloat16)
    mid_wide = mid_state.astype(jnp.float32)
    inv_two = norm_scale(mid_wide)
    gain_two = mlp_gain.astype(jnp.float32)
    mlp_in = (mid_wide * inv_two * gain_two).astype(jnp.bfloat16)
    up_all = jnp.einsum('bsh,hn->bsn', mlp_in, w_up, preferred_element_type=jnp.float32).astype(jnp.bfloat16)
    gate_val = up_all[..., :ff_width].astype(jnp.float32)
    lin_val = up_all[..., ff_width:].astype(jnp.float32)
    sigmoid_gate = jax.nn.sigmoid(gate_val)
    act_val = (gate_val * sigmoid_gate * lin_val).astype(jnp.bfloat16)
    output = (mid_wide + jnp.einsum('bsf,fh->bsh', act_val, w_down, preferred_element_type=jnp.float32)).astype(jnp.bfloat16)

    grad_w_down = jnp.einsum('bsf,bsh->fh', act_val, grad_y, preferred_element_type=jnp.float32)
    d_act = jnp.einsum('bsh,fh->bsf', grad_y, w_down, preferred_element_type=jnp.float32)
    d_gate = d_act * lin_val * sigmoid_gate * (1.0 + gate_val * (1.0 - sigmoid_gate))
    d_lin = d_act * gate_val * sigmoid_gate
    d_up = jnp.concatenate([d_gate, d_lin], axis=-1).astype(jnp.bfloat16)
    grad_w_up = jnp.einsum('bsh,bsn->hn', mlp_in, d_up, preferred_element_type=jnp.float32)
    d_mlp_in = jnp.einsum('bsn,hn->bsh', d_up, w_up, preferred_element_type=jnp.float32)
    grad_mlp_gain = jnp.sum(d_mlp_in * mid_wide * inv_two, axis=(0, 1))
    scaled_two = d_mlp_in * gain_two
    d_mid = grad_y.astype(jnp.float32) + inv_two * (scaled_two - mid_wide * inv_two * inv_two * jnp.mean(scaled_two * mid_wide, axis=-1, keepdims=True))
    d_mid_low = d_mid.astype(jnp.bfloat16)
    grad_w_out = jnp.einsum('bsn,bsh->nh', context, d_mid_low, preferred_element_type=jnp.float32)
    d_context = jnp.einsum('bsh,nh->bsn', d_mid_low, w_out, preferred_element_type=jnp.float32)
    d_context = d_context.astype(jnp.bfloat16).reshape(batch_size, seq_len, kv_heads, group_size, HEAD_DIM)
    d_query, d_key, d_values = attend_backward(q_rot, k_rot, values, attn_probs, probs_low, d_context)
    d_query = rope_turn(d_query.reshape(batch_size, seq_len, q_width // HEAD_DIM, HEAD_DIM), cos_t, -sin_t)
    d_key = rope_turn(d_key, cos_t, -sin_t)
    d_proj = jnp.concatenate([d_query.reshape(batch_size, seq_len, q_width), d_key.reshape(batch_size, seq_len, kv_width), d_values.reshape(batch_size, seq_len, kv_width)], axis=-1)
    grad_b_qkv = jnp.sum(d_proj, axis=(0, 1))
    d_proj_low = d_proj.astype(jnp.bfloat16)
    grad_w_qkv = jnp.einsum('bsh,bsn->hn', normed, d_proj_low, preferred_element_type=jnp.float32)
    d_normed = jnp.einsum('bsn,hn->bsh', d_proj_low, w_qkv, preferred_element_type=jnp.float32)
    grad_attn_gain = jnp.sum(d_normed * hid_wide * inv_one, axis=(0, 1))
    scaled_one = d_normed * gain_one
    grad_hidden = (d_mid + inv_one * (scaled_one - hid_wide * inv_one * inv_one * jnp.mean(scaled_one * hid_wide, axis=-1, keepdims=True))).astype(jnp.bfloat16)
    return output, grad_hidden, (grad_attn_gain, grad_w_qkv, grad_b_qkv, grad_w_out, grad_mlp_gain, grad_w_up, grad_w_down)


def solution(mesh):
    group_axis = mesh.axis_names[0]

    def gather_rows(weight_shard):
        return lax.all_gather(weight_shard, group_axis, axis=0, tiled=True)

    def scatter_rows(full_grad):
        return lax.psum_scatter(full_grad, group_axis, scatter_dimension=0, tiled=True)

    def local_step(hidden, positions, grad_y, attn_gain, w_qkv, b_qkv, w_out, mlp_gain, w_up, w_down):
        output, grad_hidden, full_grads = layer_pass(hidden, positions, grad_y, gather_rows(attn_gain), gather_rows(w_qkv), gather_rows(b_qkv), gather_rows(w_out), gather_rows(mlp_gain), gather_rows(w_up), gather_rows(w_down))
        return (output, grad_hidden) + tuple(scatter_rows(full_grad) for full_grad in full_grads)

    row_spec = P(group_axis)
    return jax.shard_map(local_step, mesh=mesh, in_specs=(row_spec,) * 10, out_specs=(row_spec,) * 9, check_vma=False)
```

profile of v0, /device:TPU:0, one launch (start us, length us, event | category | flops | bytes accessed | tf_op | source)
XLA Modules:
  0.0 1952.2 jit_solution(5632779717621792819)
XLA Ops:
  10.9 35.2 %all-reduce = bf16[3072]{0:T(1024)(128)(2,1)S(1)} all-reduce(bf16[3072]{0:T(1024)(128)(2,1)S(1)} %dynamic-update-slice), channel_id=1, replica_groups=mesh['fsdp'=16] {'fsdp'}, use_global_device_ids=true, to_apply=%add | all-reduce | flops 3072 | bytes 12288
  46.1 12.6 all-gather
  59.5 11.7 all-gather.1
  78.2 24.9 %broadcast_add_fusion = f32[3,512,3072]{2,1,0:T(8,128)S(1)} fusion(f32[3072]{0:T(1024)S(1)} %convert_element_type.80, bf16[2048,3072]{1,0:T(8,128)(2,1)} %all-gather.7.cloned.1.call-done, bf16[3,512,2048]{2,1,0:T(8,128)(2,1)} %param.10, f32[2048]{0:T(1024)S(1)} %bitcast.182, f32[3,512]{1,0:T(4,128)S(1)} %add_rsqrt_fusion.1), kind=kOutput, calls=%fused_computation.94 | convolution fusion | flops 19344654336 | bytes 37775360 | tf_op jit(solution)/shard_map/bsh,hn->bsn/dot_general | solution.py:65
  111.6 11.2 slice.93
  136.7 12.1 copy.137
  185.3 29.0 %fusion.111 = (f32[3,4,4,512]{3,2,1,0:T(4,128)S(1)}, f32[3,4,4,512,512]{3,4,2,1,0:T(8,128)}) fusion(pred[512,512]{0,1:T(8,128)(4,1)S(1)} %copy-done.10, bf16[3,512,4,64]{3,1,2,0:T(8,128)(2,1)} %copy.143, bf16[3,512,4,64]{3,1,2,0:T(8,128)(2,1)} %copy.78, bf16[3,512,4,4,64]{4,1,3,2,0:T(8,128)(2,1)} %bitcast.175, bf16[3,512,4,4,64]{4,1,3,2,0:T(8,128)(2,1)} %copy.82), kind=kOutput, calls=%fused_computation.145 | convolution fusion | flops 3287286272 | bytes 58556416 | tf_op jit(solution)/shard_map/sub | solution.py:37
  214.3 19.9 %fusion.87 = bf16[3,4,128,4,512]{4,2,3,1,0:T(8,128)(2,1)} fusion(bf16[3,512,4,128,1]{3,2,1,0,4:T(4,128)(2,1)S(1)} %bitcast.173, f32[3,4,4,512,512]{3,4,2,1,0:T(8,128)} %get-tuple-element.34, f32[3,4,4,512]{3,2,1,0:T(4,128)S(1)} %get-tuple-element.33), kind=kOutput, calls=%fused_computation.104 | convolution fusion | flops 3249537024 | bytes 58294272 | tf_op jit(solution)/shard_map/bkgqs,bskd->bqkgd/dot_general | solution.py:39
  234.2 21.4 %fusion.55 = (f32[3,512]{1,0:T(4,128)S(1)}, bf16[3,512,2048]{2,1,0:T(8,128)(2,1)}) fusion(bf16[3,512,2048]{1,2,0:T(8,128)(2,1)} %bitcast.192, bf16[2048,2048]{1,0:T(8,128)(2,1)} %all-gather.9.cloned.1.call-done, bf16[3,512,2048]{2,1,0:T(8,128)(2,1)} %param.10), kind=kOutput, calls=%fused_computation.79 | convolution fusion | flops 12903774208 | bytes 27269120 | tf_op jit(solution)/shard_map/bsn,nh->bsh/dot_general | solution.py:72
  255.6 60.4 %all-gather.11.cloned.1.call-done = bf16[2048,12288]{1,0:T(8,128)(2,1)} async-done(((bf16[128,12288]{1,0:T(8,128)(2,1)}), bf16[2048,12288]{1,0:T(8,128)(2,1)}) %all-gather.11.cloned.1.call-update) | async-done | bytes 50331664 | tf_op jit(solution)/shard_map/all_gather | solution.py:116
  316.0 89.5 %fusion.20 = bf16[3,512,12288]{2,1,0:T(8,128)(2,1)} fusion(bf16[2048,12288]{1,0:T(8,128)(2,1)} %all-gather.11.cloned.1.call-done, bf16[3,512,2048]{2,1,0:T(8,128)(2,1)} %get-tuple-element.36, f32[2048]{0:T(1024)S(1)} %bitcast.186, f32[3,512]{1,0:T(4,128)S(1)} %add_rsqrt_fusion), kind=kOutput, calls=%fused_computation.32 | convolution fusion | flops 77340868608 | bytes 94386176 | tf_op jit(solution)/shard_map/bsh,hn->bsn/dot_general | solution.py:77
  405.5 15.9 all-gather.13.cloned.1.call-done
  421.4 64.7 %fusion.13 = (bf16[3,512,6144]{2,1,0:T(8,128)(2,1)}, bf16[3,512,6144]{2,1,0:T(8,128)(2,1)}) fusion(bf16[3,512,12288]{2,1,0:T(8,128)(2,1)} %fusion.20, bf16[3,512,2048]{2,1,0:T(8,128)(2,1)} %param.12, bf16[6144,2048]{1,0:T(8,128)(2,1)} %all-gather.13.cloned.1.call-done), kind=kOutput, calls=%fused_computation.24 | convolution fusion | flops 38796263424 | bytes 106954752 | tf_op jit(solution)/shard_map/bsh,fh->bsf/dot_general | solution.py:85
  486.2 94.7 %fusion.59 = (f32[2048]{0:T(1024)}, f32[3,512]{1,0:T(4,128)S(1)}, f32[3,512,2048]{2,1,0:T(8,128)}) fusion(bf16[3,512,2048]{2,1,0:T(8,128)(2,1)} %get-tuple-element.36, f32[3,512]{1,0:T(4,128)S(1)} %copy-done.21, f32[2048]{0:T(1024)S(1)} %bitcast.187, bf16[2048,12288]{1,0:T(8,128)(2,1)} %all-gather.11.cloned.1.call-done, ...), kind=kOutput, calls=%fused_computation.83 | convolution fusion | flops 77406928896 | bytes 106983424 | tf_op jit(solution)/shard_map/bsn,hn->bsh/dot_general | solution.py:90
  595.2 17.8 fusion.82
  621.6 21.1 %fusion.64 = f32[3,4,128,512,1]{3,2,4,1,0:T(8,128)} fusion(bf16[3,512,4,4,128]{1,4,3,2,0:T(8,128)(2,1)} %bitcast.165, f32[3,4,4,512,512]{3,4,2,1,0:T(8,128)} %get-tuple-element.34, f32[3,4,4,512]{3,2,1,0:T(4,128)S(1)} %copy-done.25), kind=kOutput, calls=%fused_computation.90 | convolution fusion | flops 3246391296 | bytes 59867136 | tf_op jit(solution)/shard_map/bkgqs,bqkgd->bskd/dot_general | solution.py:45
  642.7 22.1 %fusion.94 = f32[3,4,512,512,4]{3,2,4,1,0:T(8,128)} fusion(bf16[3,512,4,4,128]{1,4,3,2,0:T(8,128)(2,1)} %bitcast.166, bf16[3,512,4,128,1]{3,2,1,0,4:T(4,128)(2,1)S(1)} %bitcast.174), kind=kOutput, calls=%fused_computation.119 | convolution fusion | flops 3221225472 | bytes 58195968 | tf_op jit(solution)/shard_map/bqkgd,bskd->bkgqs/dot_general | solution.py:44
  664.8 67.2 %fusion.92 = f32[3,512,4,128]{1,3,2,0:T(8,128)} fusion(f32[3,4,512,512,4]{3,2,4,1,0:T(8,128)} %fusion.94, bf16[3,512,4,4,64]{4,1,3,2,0:T(8,128)(2,1)} %bitcast.176, bf16[3,512,4,4,64]{4,1,3,2,0:T(8,128)(2,1)} %copy.82, f32[3,4,4,512,512]{3,4,2,1,0:T(8,128)} %get-tuple-element.34, f32[3,4,4,512]{3,2,1,0:T(4,128)S(1)} %copy-done.25), kind=kOutput, calls=%fused_computation.115 | convolution fusion | flops 3321913856 | bytes 110198784 | tf_op jit(solution)/shard_map/bkgqs,bqkgd->bskd/dot_general | solution.py:49
  731.9 67.7 %fusion.32 = f32[3,4,128,4,512]{4,2,3,1,0:T(8,128)} fusion(f32[3,4,512,512,4]{3,2,4,1,0:T(8,128)} %fusion.94, bf16[3,512,4,64]{3,1,2,0:T(8,128)(2,1)} %copy.143, bf16[3,512,4,64]{3,1,2,0:T(8,128)(2,1)} %copy.78, f32[3,4,4,512,512]{3,4,2,1,0:T(8,128)} %get-tuple-element.34, f32[3,4,4,512]{3,2,1,0:T(4,128)S(1)} %copy-done.25), kind=kOutput, calls=%fused_computation.54 | convolution fusion | flops 3312476672 | bytes 114917376 | tf_op jit(solution)/shard_map/bkgqs,bskd->bqkgd/dot_general | solution.py:48
  837.3 12.5 pad_maximum_fusion.4
  849.8 12.6 copy.92
  862.4 13.8 reshape.132
  876.2 29.5 %convolution_bitcast_fusion.2 = f32[2048,3072]{1,0:T(8,128)} fusion(bf16[3,512,2048]{2,1,0:T(8,128)(2,1)} %param.10, f32[2048]{0:T(1024)S(1)} %bitcast.183, f32[3,512]{1,0:T(4,128)S(1)} %copy-done.15, f32[3,512,512]{2,1,0:T(8,128)S(1)} %copy-done.2, f32[3,512,512]{2,1,0:T(8,128)} %copy.100, f32[3,512,2048]{2,1,0:T(8,128)} %reshape.132), kind=kOutput, calls=%fused_computation.62 | convolution fusion | flops 19368247296 | bytes 50345984 | tf_op jit(solution)/shard_map/bsh,bsn->hn/dot_general | solution.py:104
  905.8 21.6 %convolution_bitcast_fusion.3 = f32[2048,2048]{1,0:T(8,128)} fusion(bf16[3,512,2048]{1,2,0:T(8,128)(2,1)} %bitcast.193, f32[3,512,2048]{2,1,0:T(8,128)} %copy-done), kind=kOutput, calls=%fused_computation.95 | convolution fusion | flops 12888047616 | bytes 35651584 | tf_op jit(solution)/shard_map/bsn,bsh->nh/dot_general | solution.py:95
  927.4 53.0 %convolution_bitcast_fusion.1 = f32[6144,2048]{1,0:T(8,128)} fusion(bf16[3,512,2048]{2,1,0:T(8,128)(2,1)} %param.12, bf16[3,512,12288]{2,1,0:T(8,128)(2,1)} %fusion.20), kind=kOutput, calls=%fused_computation.33 | convolution fusion | flops 38730203136 | bytes 94371840 | tf_op jit(solution)/shard_map/bsf,bsh->fh/dot_general | solution.py:84
  981.1 91.6 %convolution_bitcast_fusion = f32[2048,12288]{1,0:T(8,128)} fusion(bf16[3,512,6144]{2,1,0:T(8,128)(2,1)} %get-tuple-element.17, bf16[3,512,6144]{2,1,0:T(8,128)(2,1)} %get-tuple-element.16, bf16[3,512,2048]{2,1,0:T(8,128)(2,1)} %get-tuple-element.36, f32[2048]{0:T(1024)S(1)} %bitcast.189, f32[3,512]{1,0:T(4,128)S(1)} %copy-done.22), kind=kOutput, calls=%fused_computation.6 | convolution fusion | flops 77397491712 | bytes 144717824 | tf_op jit(solution)/shard_map/bsh,bsn->hn/dot_general | solution.py:89
  1081.4 30.6 %fusion.54 = (f32[2048]{0:T(1024)S(1)}, f32[3,512]{1,0:T(4,128)S(1)}, f32[3,512,2048]{2,1,0:T(8,128)}) fusion(bf16[3,512,2048]{2,1,0:T(8,128)(2,1)} %param.10, f32[3,512]{1,0:T(4,128)S(1)} %copy-done.16, f32[2048]{0:T(1024)S(1)} %bitcast.184, bf16[2048,3072]{1,0:T(8,128)(2,1)} %all-gather.7.cloned.1.call-done, f32[3,512,512]{2,1,0:T(8,128)S(1)} %copy-done.3, ...), kind=kOutput, calls=%fused_computation.78 | convolution fusion | flops 19377680384 | bytes 50360320 | tf_op jit(solution)/shard_map/bsn,hn->bsh/dot_general | solution.py:105
  1112.0 33.1 %all-reduce.5 = (f32[2048]{0:T(1024)S(1)}, f32[3072]{0:T(1024)S(1)}, f32[2048]{0:T(1024)S(1)}) all-reduce(f32[2048]{0:T(1024)S(1)} %get-tuple-element.11, f32[3072]{0:T(1024)S(1)} %fusion.37, f32[2048]{0:T(1024)S(1)} %copy-done.23), channel_id=2, replica_groups=mesh['fsdp'=16] {'fsdp'}, use_global_device_ids=true, to_apply=%region_8.9.clone | all-reduce | flops 7168 | bytes 57344
  1146.9 14.2 fusion.49
  1161.1 55.9 %fusion.56 = bf16[3,512,2048]{2,1,0:T(8,128)(2,1)} fusion(bf16[3,512,2048]{2,1,0:T(8,128)(2,1)} %get-tuple-element.36, bf16[6144,2048]{1,0:T(8,128)(2,1)} %all-gather.13.cloned.1.call-done, bf16[3,512,12288]{2,1,0:T(8,128)(2,1)} %fusion.20), kind=kOutput, calls=%fused_computation.80 | convolution fusion | flops 38739640320 | bytes 75497472 | tf_op jit(solution)/shard_map/bsf,fh->bsh/dot_general | solution.py:82
  1225.2 250.2 %reduce-scatter.11.cloned.1.call-done = f32[384,2048]{1,0:T(8,128)} async-done(((f32[6144,2048]{1,0:T(8,128)}), f32[384,2048]{1,0:T(8,128)}) %reduce-scatter.11.cloned.1.call-update) | async-done | bytes 3145744 | tf_op jit(solution)/shard_map/reduce_scatter | solution.py:119
  1475.4 469.5 %reduce-scatter.13.cloned.1.call-done = f32[128,12288]{1,0:T(8,128)} async-done(((f32[2048,12288]{1,0:T(8,128)}), f32[128,12288]{1,0:T(8,128)}) %reduce-scatter.13.cloned.1.call-update) | async-done | bytes 6291472
  (122 shorter events, 150.0 us)
Async XLA Ops:
  7.2 71.0 %all-gather.7.cloned.1.call-start = ((), (), s32[]{:S(2)}) async-start(), calls=%async_computation.4 | async-start | bytes 13369344 | tf_op jit(solution)/shard_map/all_gather | solution.py:116
  7.9 226.3 %all-gather.9.cloned.1.call-start = ((), (), s32[]{:S(2)}) async-start(), calls=%async_computation.5 | async-start | bytes 8912896 | tf_op jit(solution)/shard_map/all_gather | solution.py:116
  8.7 307.3 %all-gather.11.cloned.1.call-start = ((), (), s32[]{:S(2)}) async-start(), calls=%async_computation.6 | async-start | bytes 53477376 | tf_op jit(solution)/shard_map/all_gather | solution.py:116
  9.4 412.1 %all-gather.13.cloned.1.call-start = ((), (), s32[]{:S(2)}) async-start(), calls=%async_computation.7 | async-start | bytes 26738688 | tf_op jit(solution)/shard_map/all_gather | solution.py:116
  10.0 1207.1 %reduce-scatter.7.cloned.1.call-start = ((), (), s32[]{:S(2)}) async-start(), calls=%async_computation.8 | async-start | bytes 26738688 | tf_op jit(solution)/shard_map/reduce_scatter | solution.py:119
  58.8 19.4 copy-start.11
  76.7 1.5 copy-start.14
  78.2 92.0 %copy-start.6 = (f32[3,512,32]{1,2,0:T(8,128)}, f32[3,512,32]{1,2,0:T(8,128)S(1)}, u32[]{:S(2)}) copy-start(f32[3,512,32]{1,2,0:T(8,128)S(1)} %get-tuple-element.32) | copy-start | bytes 589828
  103.1 6.4 copy-start.1
  174.4 10.8 copy-start.10
  185.3 29.0 %copy-start.4 = (bf16[3,512,4,128]{3,2,1,0:T(4,128)(2,1)S(1)}, bf16[3,512,4,128]{3,2,1,0:T(4,128)(2,1)}, u32[]{:S(2)}) copy-start(bf16[3,512,4,128]{3,2,1,0:T(4,128)(2,1)} %convert_element_type.81) | copy-start | bytes 4718596
  214.2 19.9 %copy-start.24 = (f32[3,4,4,512]{3,2,1,0:T(4,128)}, f32[3,4,4,512]{3,2,1,0:T(4,128)S(1)}, u32[]{:S(2)}) copy-start(f32[3,4,4,512]{3,2,1,0:T(4,128)S(1)} %get-tuple-element.33) | copy-start | bytes 294916
  234.2 81.8 %copy-start.17 = (f32[16,1,128]{2,1,0:T(1,128)S(1)}, f32[16,1,128]{2,1,0:T(1,128)}, u32[]{:S(2)}) copy-start(f32[16,1,128]{2,1,0:T(1,128)} %convert_element_type.102) | copy-start | bytes 24580
  255.6 150.0 %copy-start.20 = (f32[3,512]{1,0:T(4,128)}, f32[3,512]{1,0:T(4,128)S(1)}, u32[]{:S(2)}) copy-start(f32[3,512]{1,0:T(4,128)S(1)} %add_rsqrt_fusion) | copy-start | bytes 18436
  421.4 64.7 %copy-start.18 = (f32[16,1,128]{2,1,0:T(1,128)S(1)}, f32[16,1,128]{2,1,0:T(1,128)}, u32[]{:S(2)}) copy-start(f32[16,1,128]{2,1,0:T(1,128)} %convert_element_type.102) | copy-start | bytes 24580
  421.4 64.7 %copy-start.21 = (f32[3,512]{1,0:T(4,128)S(1)}, f32[3,512]{1,0:T(4,128)}, u32[]{:S(2)}) copy-start(f32[3,512]{1,0:T(4,128)} %copy-done.20) | copy-start | bytes 18436
  590.7 4.5 copy-start
  613.0 8.6 copy-start.25
  621.6 21.1 %copy-start.5 = (bf16[3,512,4,128]{3,2,1,0:T(4,128)(2,1)S(1)}, bf16[3,512,4,128]{3,2,1,0:T(4,128)(2,1)}, u32[]{:S(2)}) copy-start(bf16[3,512,4,128]{3,2,1,0:T(4,128)(2,1)} %convert_element_type.81) | copy-start | bytes 4718596
  731.9 67.7 %copy-start.8 = (f32[3,4,128,512,1]{3,2,4,1,0:T(8,128)S(1)}, f32[3,4,128,512,1]{3,2,4,1,0:T(8,128)}, u32[]{:S(2)}) copy-start(f32[3,4,128,512,1]{3,2,4,1,0:T(8,128)} %fusion.64) | copy-start | bytes 9437188
  799.6 5.6 copy-start.7
  799.6 5.6 copy-start.9
  862.4 13.8 copy-start.2
  862.4 13.8 copy-start.12
  862.4 13.8 copy-start.15
  905.7 319.5 %reduce-scatter.9.cloned.1.call-start = ((), (), s32[]{:S(2)}) async-start(), calls=%async_computation.9 | async-start | bytes 17825792 | tf_op jit(solution)/shard_map/reduce_scatter | solution.py:119
  927.4 548.1 %reduce-scatter.11.cloned.1.call-start = ((), (), s32[]{:S(2)}) async-start(), calls=%async_computation.10 | async-start | bytes 53477376 | tf_op jit(solution)/shard_map/reduce_scatter | solution.py:119
  980.4 964.5 %reduce-scatter.13.cloned.1.call-start = ((), (), s32[]{:S(2)}) async-start(), calls=%async_computation.11 | async-start | bytes 106954752
  1072.7 1.9 copy-start.3
  1072.7 8.6 copy-start.13
  1072.7 8.6 copy-start.16
  1081.3 30.7 %copy-start.23 = (f32[2048]{0:T(1024)S(1)}, f32[2048]{0:T(1024)}, u32[]{:S(2)}) copy-start(f32[2048]{0:T(1024)} %get-tuple-element.9) | copy-start | bytes 24580
  (2 other events, 1.4 us)
Sparse Core Ops, SparseCore 0:
  10.2 66.4 all-gather.6
  78.9 48.6 all-gather.8
  129.8 186.1 all-gather.10
  318.1 103.3 all-gather.12
  905.8 137.6 reduce-scatter.6
  1046.3 178.8 reduce-scatter.8
  1230.7 244.6 reduce-scatter.10
  1480.9 463.9 reduce-scatter.12
where the time goes:
time: 1960 us; the launch traced here: 1950 us
  matrix products  822 us (42%)
  waiting for transfers between devices  807 us (41%)
  local copies, waits for them, and re-layouts  151 us (8%)
  blocking collectives  92.7 us (5%)
  other arithmetic  64.7 us (3%)
    unnamed x9, waiting for transfers between devices  472 us
    reduce_scatter x3, waiting for transfers between devices, scatter_rows(): lax.psum_scatter(full_grad, group_axis, scatter_dimension=0, tiled=True)  258 us
    dot_general x1, matrix products, layer_pass(): jnp.einsum('bsn,hn->bsh', d_up, w_up, preferred_element_type=jnp.float32)  94.7 us
    dot_general x1, matrix products, layer_pass(): jnp.einsum('bsh,bsn->hn', mlp_in, d_up, preferred_element_type=jnp.float32)  91.6 us
    dot_general x1, matrix products, layer_pass(): jnp.einsum('bsh,hn->bsn', mlp_in, w_up, preferred_element_type=jnp.float32)  89.5 us
    all_gather x4, waiting for transfers between devices, gather_rows(): return lax.all_gather(weight_shard, group_axis, axis=0, tiled=True)  76.4 us
    unnamed x2, blocking collectives  68.3 us
    dot_general x1, matrix products, attend_backward(): jnp.einsum('bkgqs,bskd->bqkgd', d_scores, k_rot, preferred_element_type=j...  67.7 us
  transfers between devices with their start and end apart: 8, of which 5 were waited for; matrix products, arithmetic and copies ran while one was open for 28% of the time, Pallas kernels for 0%

commit v1 on v0

v1 whole, which is shorter than its diff:
```python
import jax
import jax.numpy as jnp
from jax import lax
from jax.sharding import PartitionSpec as P

HEAD_DIM = 128
ROPE_BASE = 10000.0
EPS = 1e-5


def norm_scale(rows_in):
    return lax.rsqrt(jnp.mean(rows_in * rows_in, axis=-1, keepdims=True) + EPS)


def rope_tables(positions):
    rot_dim = HEAD_DIM // 2
    inv_freq = 1.0 / (ROPE_BASE ** (jnp.arange(0, rot_dim, 2, dtype=jnp.float32) / rot_dim))
    angles = positions.astype(jnp.float32)[:, :, None, None] * inv_freq
    return jnp.cos(angles), jnp.sin(angles)


def rope_turn(head_vals, cos_t, sin_t):
    rot_dim = HEAD_DIM // 2
    lead_shape = head_vals.shape[:-1]
    rot_pairs = head_vals[..., :rot_dim].reshape(lead_shape + (rot_dim // 2, 2))
    even_part = rot_pairs[..., 0]
    odd_part = rot_pairs[..., 1]
    turned = jnp.stack([even_part * cos_t - odd_part * sin_t, odd_part * cos_t + even_part * sin_t], axis=-1)
    return jnp.concatenate([turned.reshape(lead_shape + (rot_dim,)), head_vals[..., rot_dim:]], axis=-1)


def attend_forward(q_rot, k_rot, values):
    seq_len = q_rot.shape[1]
    token_index = jnp.arange(seq_len)
    causal = token_index[:, None] >= token_index[None, :]
    scores = jnp.einsum('bqkgd,bskd->bkgqs', q_rot, k_rot, preferred_element_type=jnp.float32) * HEAD_DIM ** -0.5
    attn_probs = jax.nn.softmax(jnp.where(causal, scores, -1e30), axis=-1)
    probs_low = attn_probs.astype(jnp.bfloat16)
    context = jnp.einsum('bkgqs,bskd->bqkgd', probs_low, values, preferred_element_type=jnp.float32)
    return context.astype(jnp.bfloat16), attn_probs, probs_low


def attend_backward(q_rot, k_rot, values, attn_probs, probs_low, d_context):
    d_probs = jnp.einsum('bqkgd,bskd->bkgqs', d_context, values, preferred_element_type=jnp.float32)
    d_values = jnp.einsum('bkgqs,bqkgd->bskd', probs_low, d_context, preferred_element_type=jnp.float32)
    d_scores = attn_probs * (d_probs - jnp.sum(attn_probs * d_probs, axis=-1, keepdims=True)) * HEAD_DIM ** -0.5
    d_scores = d_scores.astype(jnp.bfloat16)
    d_query = jnp.einsum('bkgqs,bskd->bqkgd', d_scores, k_rot, preferred_element_type=jnp.float32)
    d_key = jnp.einsum('bkgqs,bqkgd->bskd', d_scores, q_rot, preferred_element_type=jnp.float32)
    return d_query, d_key, d_values


def own_blocks(rows_in, width, bit):
    return jnp.concatenate([lax.dynamic_slice_in_dim(rows_in, (2 * i + bit) * width, width, axis=1) for i in range(8)], axis=1)


def outer_sum(own_left, own_right, far_left, far_right):
    first = lax.dot_general(own_left, own_right, CONTRACT_ROWS, preferred_element_type=jnp.float32)
    return first + lax.dot_general(far_left, far_right, CONTRACT_ROWS, preferred_element_type=jnp.float32)


CONTRACT_ROWS = (((0,), (0,)), ((), ()))
CONTRACT_COLS = (((1,), (1,)), ((), ()))


def layer_pass(axis, hidden, positions, grad_y, attn_gain_s, w_qkv_s, b_qkv_s, w_out_s, mlp_gain_s, w_up_s, w_down_s):
    batch_size, seq_len, width = hidden.shape
    tokens = batch_size * seq_len
    count = lax.axis_size(axis)
    bit = lax.axis_index(axis) % 2
    swap = [(i, i ^ 1) for i in range(count)]
    groups = [list(range(0, count, 2)), list(range(1, count, 2))]

    def far(value):
        return lax.ppermute(value, axis, swap)

    def scatter(chip_sum):
        return lax.psum_scatter(chip_sum, axis, scatter_dimension=0, axis_index_groups=groups, tiled=True)

    def gather(shard):
        return lax.all_gather(shard, axis, axis=0, tiled=True)

    gain_rows = attn_gain_s.shape[0]
    bias_rows = b_qkv_s.shape[0]
    packed = jnp.concatenate([attn_gain_s, mlp_gain_s, b_qkv_s, jnp.zeros((4 * 128 - 2 * gain_rows - bias_rows,), jnp.bfloat16)])
    packed = lax.all_gather(packed.reshape(1, 4, 128), axis, axis=0, tiled=True).reshape(count, 512)
    attn_gain = packed[:, :gain_rows].reshape(width)
    mlp_gain = packed[:, gain_rows:2 * gain_rows].reshape(width)
    b_qkv = packed[:, 2 * gain_rows:2 * gain_rows + bias_rows].reshape(bias_rows * count)
    w_qkv = gather(w_qkv_s)
    w_out = gather(w_out_s)
    w_up = gather(w_up_s)
    w_down = gather(w_down_s)

    q_width = w_out.shape[0]
    kv_width = (w_qkv.shape[1] - q_width) // 2
    kv_heads = kv_width // HEAD_DIM
    group_size = q_width // kv_width
    ff_width = w_down.shape[0]
    cos_t, sin_t = rope_tables(positions)
    dy = grad_y.reshape(tokens, width)
    hid_wide = hidden.reshape(tokens, width).astype(jnp.float32)
    inv_one = norm_scale(hid_wide)
    gain_one = attn_gain.astype(jnp.float32)
    normed = (hid_wide * inv_one * gain_one).astype(jnp.bfloat16)
    far_dy = far(dy)
    qkv_proj = jnp.dot(normed, w_qkv, preferred_element_type=jnp.float32) + b_qkv.astype(jnp.float32)
    qkv_proj = qkv_proj.reshape(batch_size, seq_len, -1)
    q_rot = rope_turn(qkv_proj[..., :q_width].reshape(batch_size, seq_len, q_width // HEAD_DIM, HEAD_DIM), cos_t, sin_t)
    q_rot = q_rot.astype(jnp.bfloat16).reshape(batch_size, seq_len, kv_heads, group_size, HEAD_DIM)
    k_rot = rope_turn(qkv_proj[..., q_width:q_width + kv_width].reshape(batch_size, seq_len, kv_heads, HEAD_DIM), cos_t, sin_t).astype(jnp.bfloat16)
    values = qkv_proj[..., q_width + kv_width:].reshape(batch_size, seq_len, kv_heads, HEAD_DIM).astype(jnp.bfloat16)
    context, attn_probs, probs_low = attend_forward(q_rot, k_rot, values)
    context = context.reshape(tokens, q_width)
    mid_state = (hid_wide + jnp.dot(context, w_out, preferred_element_type=jnp.float32)).astype(jnp.bfloat16)
    mid_wide = mid_state.astype(jnp.float32)
    inv_two = norm_scale(mid_wide)
    gain_two = mlp_gain.astype(jnp.float32)
    mlp_in = (mid_wide * inv_two * gain_two).astype(jnp.bfloat16)
    up_all = jnp.dot(mlp_in, w_up, preferred_element_type=jnp.float32).astype(jnp.bfloat16)
    gate_val = up_all[..., :ff_width].astype(jnp.float32)
    lin_val = up_all[..., ff_width:].astype(jnp.float32)
    sigmoid_gate = jax.nn.sigmoid(gate_val)
    act_val = (gate_val * sigmoid_gate * lin_val).astype(jnp.bfloat16)

    ff_rows = ff_width // count
    own_act = own_blocks(act_val, ff_rows, bit)
    far_act = far(own_blocks(act_val, ff_rows, 1 - bit))
    chip_w_down = outer_sum(own_act, dy, far_act, far_dy)
    chip_w_down, dy_next = lax.optimization_barrier((chip_w_down, dy))
    grad_w_down = scatter(chip_w_down)

    d_act = lax.dot_general(dy_next, w_down, CONTRACT_COLS, preferred_element_type=jnp.float32)
    d_gate = (d_act * lin_val * sigmoid_gate * (1.0 + gate_val * (1.0 - sigmoid_gate))).astype(jnp.bfloat16)
    d_lin = (d_act * gate_val * sigmoid_gate).astype(jnp.bfloat16)
    far_gate = far(d_gate)
    far_lin = far(d_lin)
    h_rows = width // count
    own_mlp = own_blocks(mlp_in, h_rows, bit)
    far_mlp = far(own_blocks(mlp_in, h_rows, 1 - bit))
    d_up = jnp.concatenate([d_gate, d_lin], axis=-1)
    far_up = jnp.concatenate([far_gate, far_lin], axis=-1)
    chip_w_up = outer_sum(own_mlp, d_up, far_mlp, far_up)
    chip_w_up, d_up_next = lax.optimization_barrier((chip_w_up, d_up))
    grad_w_up = scatter(chip_w_up)

    d_mlp_in = lax.dot_general(d_up_next, w_up, CONTRACT_COLS, preferred_element_type=jnp.float32)
    grad_mlp_gain = jnp.sum(d_mlp_in * mid_wide * inv_two, axis=0)
    scaled_two = d_mlp_in * gain_two
    d_mid = dy.astype(jnp.float32) + inv_two * (scaled_two - mid_wide * inv_two * inv_two * jnp.mean(scaled_two * mid_wide, axis=-1, keepdims=True))
    d_mid_low = d_mid.astype(jnp.bfloat16)
    far_mid = far(d_mid_low)
    own_ctx = own_blocks(context, q_width // count, bit)
    far_ctx = far(own_blocks(context, q_width // count, 1 - bit))
    d_context = lax.dot_general(d_mid_low, w_out, CONTRACT_COLS, preferred_element_type=jnp.float32)
    d_context = d_context.astype(jnp.bfloat16)
    chip_w_out = outer_sum(own_ctx, d_mid_low, far_ctx, far_mid)
    chip_w_out, d_context = lax.optimization_barrier((chip_w_out, d_context))
    grad_w_out = scatter(chip_w_out)
    d_context = d_context.reshape(batch_size, seq_len, kv_heads, group_size, HEAD_DIM)
    d_query, d_key, d_values = attend_backward(q_rot, k_rot, values, attn_probs, probs_low, d_context)
    d_query = rope_turn(d_query.reshape(batch_size, seq_len, q_width // HEAD_DIM, HEAD_DIM), cos_t, -sin_t)
    d_key = rope_turn(d_key, cos_t, -sin_t)
    d_proj = jnp.concatenate([d_query.reshape(tokens, q_width), d_key.reshape(tokens, kv_width), d_values.reshape(tokens, kv_width)], axis=-1)
    grad_b_qkv = jnp.sum(d_proj, axis=0)
    d_proj_low = d_proj.astype(jnp.bfloat16)
    far_proj = far(d_proj_low)
    own_normed = own_blocks(normed, h_rows, bit)
    far_normed = far(own_blocks(normed, h_rows, 1 - bit))
    chip_w_qkv = outer_sum(own_normed, d_proj_low, far_normed, far_proj)
    chip_w_qkv, d_proj_next, act_next = lax.optimization_barrier((chip_w_qkv, d_proj_low, act_val))
    grad_w_qkv = scatter(chip_w_qkv)
    d_normed = lax.dot_general(d_proj_next, w_qkv, CONTRACT_COLS, preferred_element_type=jnp.float32)
    grad_attn_gain = jnp.sum(d_normed * hid_wide * inv_one, axis=0)
    scaled_one = d_normed * gain_one
    grad_hidden = (d_mid + inv_one * (scaled_one - hid_wide * inv_one * inv_one * jnp.mean(scaled_one * hid_wide, axis=-1, keepdims=True))).astype(jnp.bfloat16)
    output = (mid_wide + jnp.dot(act_next, w_down, preferred_element_type=jnp.float32)).astype(jnp.bfloat16)

    small = [lax.psum_scatter(value, axis, scatter_dimension=0, tiled=True) for value in (grad_attn_gain, grad_b_qkv, grad_mlp_gain)]
    whole = (batch_size, seq_len, width)
    return output.reshape(whole), grad_hidden.reshape(whole), small[0], grad_w_qkv, small[1], grad_w_out, small[2], grad_w_up, grad_w_down


def solution(mesh):
    group_axis = mesh.axis_names[0]

    def local_step(*args):
        return layer_pass(group_axis, *args)

    row_spec = P(group_axis)
    return jax.shard_map(local_step, mesh=mesh, in_specs=(row_spec,) * 10, out_specs=(row_spec,) * 9, check_vma=False)
```

time: 1960 us -> 1670 us (0.85)
  waiting for transfers between devices: 807 us -> 403 us
  local copies, waits for them, and re-layouts: 151 us -> 238 us
  other arithmetic: 64.7 us -> 136 us
  blocking collectives: 92.7 us -> 47.9 us
    unnamed x9 -> x8, waiting for transfers between devices: 472 us -> 3.83 us
    reduce_scatter x3 -> x4, waiting for transfers between devices: 258 us -> 327 us  [scatter(): lax.psum_scatter(chip_sum, axis, scatter_dimension=0, axis_index_groups=g...]
    convert_element_type x1 -> x4, other arithmetic: 0.01 us -> 43.1 us  [the longest x1 18.3 us: layer_pass(): act_val = (gate_val * sigmoid_gate * lin_val).astype(jnp.bfloat16)]
    unnamed x63 -> x120, local copies, waits for them, and re-layouts: 55.3 us -> 95.9 us
    unnamed x2 -> x1, blocking collectives: 68.3 us -> 33.4 us
    concatenate x0 -> x1, other arithmetic: none -> 25.4 us  [layer_pass(): d_up = jnp.concatenate([d_gate, d_lin], axis=-1)]
    dot_general x12 -> x16, matrix products: 595 us -> 592 us  [the longest x4 110 us: outer_sum(): lax.dot_general(far_left, far_right, CONTRACT_ROWS, preferred_element_typ...]
  transfers between devices with their start and end apart: 8 -> 17, of which waited for: 5 -> 4; matrix products, arithmetic and copies ran while one was open for 28% -> 57% of each run, Pallas kernels for 0% -> 0%
where the time goes in v1:
time: 1670 us; the launch traced here: 1660 us
  matrix products  819 us (49%)
  waiting for transfers between devices  403 us (24%)
  local copies, waits for them, and re-layouts  238 us (14%)
  other arithmetic  136 us (8%)
  blocking collectives  47.9 us (3%)
    reduce_scatter x4, waiting for transfers between devices, scatter(): lax.psum_scatter(chip_sum, axis, scatter_dimension=0, axis_index_groups=g...  327 us
    dot_general x4, matrix products, outer_sum(): lax.dot_general(far_left, far_right, CONTRACT_ROWS, preferred_element_typ...  110 us
    unnamed x120, local copies, waits for them, and re-layouts  95.9 us
    dot_general x4, matrix products, outer_sum(): lax.dot_general(own_left, own_right, CONTRACT_ROWS, preferred_element_typ...  95.1 us
    dot_general x1, matrix products, layer_pass(): lax.dot_general(d_up_next, w_up, CONTRACT_COLS, preferred_element_type=jn...  92.9 us
    dot_general x1, matrix products, layer_pass(): jnp.dot(mlp_in, w_up, preferred_element_type=jnp.float32)  86.8 us
    all_gather x4, waiting for transfers between devices, gather(): return lax.all_gather(shard, axis, axis=0, tiled=True)  70.3 us
    dot_general x1, matrix products, attend_backward(): jnp.einsum('bkgqs,bskd->bqkgd', d_scores, k_rot, preferred_element_type=j...  67.8 us
  transfers between devices with their start and end apart: 17, of which 4 were waited for; matrix products, arithmetic and copies ran while one was open for 57% of the time, Pallas kernels for 0%

profile of v1, /device:TPU:0, one launch (start us, length us, event | category | flops | bytes accessed | tf_op | source)
XLA Modules:
  0.0 1660.8 jit_solution(12990231088397717190)
XLA Ops:
  10.8 14.5 all_gather.15
  39.3 36.1 %all-gather.5.cloned.1.call-done = bf16[2048,3072]{1,0:T(8,128)(2,1)} async-done(((bf16[128,3072]{1,0:T(8,128)(2,1)}), bf16[2048,3072]{1,0:T(8,128)(2,1)}) %all-gather.5.cloned.1.call-update) | async-done | bytes 12582928 | tf_op jit(solution)/shard_map/all_gather | solution.py:81
  75.4 24.8 %convolution_add_fusion = f32[1536,3072]{1,0:T(8,128)S(1)} fusion(bf16[1536,2048]{1,0:T(8,128)(2,1)} %fusion.43, bf16[2048,3072]{1,0:T(8,128)(2,1)} %all-gather.5.cloned.1.call-done, f32[3072]{0:T(1024)S(1)} %reshape.196), kind=kOutput, calls=%fused_computation.47 | convolution fusion | flops 19332071424 | bytes 37761024 | tf_op jit(solution)/shard_map/dot_general | solution.py:107
  126.2 12.6 copy.138
  184.2 28.2 %fusion.81 = (f32[3,4,4,512]{3,2,1,0:T(4,128)S(1)}, f32[3,4,4,512,512]{3,4,2,1,0:T(8,128)}) fusion(pred[512,512]{0,1:T(8,128)(4,1)S(1)} %copy-done.14, bf16[3,512,4,64]{3,1,2,0:T(8,128)(2,1)S(1)} %copy-done.12, bf16[3,512,4,64]{3,1,2,0:T(8,128)(2,1)} %copy.94, bf16[3,512,4,4,64]{4,1,3,2,0:T(8,128)(2,1)} %bitcast.221, bf16[3,512,4,4,64]{4,1,3,2,0:T(8,128)(2,1)} %copy.99), kind=kOutput, calls=%fused_computation.201 | convolution fusion | flops 3287286272 | bytes 58556416 | tf_op jit(solution)/shard_map/sub | solution.py:37
  212.5 20.1 %convert_bitcast_fusion = bf16[3,512,4,4,128]{1,4,3,2,0:T(8,128)(2,1)} fusion(bf16[3,512,4,128,1]{1,3,4,2,0:T(8,128)(2,1)S(1)} %bitcast.216, f32[3,4,4,512,512]{3,4,2,1,0:T(8,128)} %get-tuple-element.120, f32[3,4,4,512]{3,2,1,0:T(4,128)S(1)} %get-tuple-element.119), kind=kOutput, calls=%fused_computation.87 | convolution fusion | flops 3249537024 | bytes 58294272 | tf_op jit(solution)/shard_map/bkgqs,bskd->bqkgd/dot_general | solution.py:39
  254.9 18.7 %fusion.36 = (f32[1536]{0:T(1024)S(1)}, bf16[1536,2048]{1,0:T(8,128)(2,1)S(1)}) fusion(bf16[1536,2048]{1,0:T(8,128)(2,1)} %reshape.181, bf16[2048,2048]{1,0:T(8,128)(2,1)} %all-gather.7.cloned.1.call-done, bf16[3,512,2048]{2,1,0:T(8,128)(2,1)} %param.10), kind=kOutput, calls=%fused_computation.54 | convolution fusion | flops 12903774208 | bytes 27269120 | tf_op jit(solution)/shard_map/dot_general | solution.py:115
  280.5 34.2 %all-gather.9.cloned.1.call-done = bf16[2048,12288]{1,0:T(8,128)(2,1)} async-done(((bf16[128,12288]{1,0:T(8,128)(2,1)}), bf16[2048,12288]{1,0:T(8,128)(2,1)}) %all-gather.9.cloned.1.call-update) | async-done | bytes 50331664 | tf_op jit(solution)/shard_map/all_gather | solution.py:81
  314.8 86.8 %convolution_convert_fusion = bf16[1536,12288]{1,0:T(8,128)(2,1)} fusion(bf16[1536,2048]{1,0:T(8,128)(2,1)} %fusion.31, bf16[2048,12288]{1,0:T(8,128)(2,1)} %all-gather.9.cloned.1.call-done), kind=kOutput, calls=%fused_computation.15 | convolution fusion | flops 77328285696 | bytes 94371840 | tf_op jit(solution)/shard_map/dot_general | solution.py:120
  401.6 18.3 %fusion.6 = bf16[1536,6144]{1,0:T(8,128)(2,1)S(1)} fusion(bf16[1536,12288]{1,0:T(8,128)(2,1)} %convolution_convert_fusion), kind=kLoop, calls=%fused_computation.17 | loop fusion | flops 75497472 | bytes 56623104 | tf_op jit(solution)/shard_map/convert_element_type | solution.py:124
  434.4 24.8 %fusion.82 = f32[3072,2048]{1,0:T(8,128)} fusion(bf16[1536,3072]{1,0:T(8,128)(2,1)} %get-tuple-element.39, bf16[1536,2048]{1,0:T(8,128)(2,1)S(1)} %bitcast.209), kind=kOutput, calls=%fused_computation.202 | convolution fusion | flops 19327352832 | bytes 40894464 | tf_op jit(solution)/shard_map/dot_general | solution.py:58
  461.8 30.6 %convolution_add_fusion.1 = f32[3072,2048]{1,0:T(8,128)} fusion(f32[3072,2048]{1,0:T(8,128)} %fusion.82, bf16[1536,3072]{1,0:T(8,128)(2,1)} %collective-permute-done, bf16[1536,2048]{1,0:T(8,128)(2,1)} %copy-done.32), kind=kOutput, calls=%fused_computation.48 | convolution fusion | flops 19333644288 | bytes 66060288 | tf_op jit(solution)/shard_map/dot_general | solution.py:59
  492.3 65.0 %fusion.9 = (bf16[1536,6144]{1,0:T(8,128)(2,1)}, bf16[1536,6144]{1,0:T(8,128)(2,1)}) fusion(bf16[1536,12288]{1,0:T(8,128)(2,1)} %convolution_convert_fusion, bf16[1536,2048]{1,0:T(8,128)(2,1)} %bitcast.205, bf16[6144,2048]{1,0:T(8,128)(2,1)} %all-gather.11.cloned.1.call-done), kind=kOutput, calls=%fused_computation.20 | convolution fusion | flops 38796263424 | bytes 106954752 | tf_op jit(solution)/shard_map/dot_general | solution.py:133
  571.4 48.7 %fusion.77 = f32[1024,12288]{1,0:T(8,128)} fusion(bf16[1536,1024]{1,0:T(8,128)(2,1)} %copy-done.29, bf16[1536,6144]{1,0:T(8,128)(2,1)} %get-tuple-element.35, bf16[1536,6144]{1,0:T(8,128)(2,1)} %get-tuple-element.34), kind=kOutput, calls=%fused_computation.197 | convolution fusion | flops 38730203136 | bytes 91226112 | tf_op jit(solution)/shard_map/dot_general | solution.py:58
  620.1 25.4 %pad_maximum_fusion = bf16[1536,12288]{1,0:T(8,128)(2,1)} fusion(bf16[1536,6144]{1,0:T(8,128)(2,1)} %get-tuple-element.35, bf16[1536,6144]{1,0:T(8,128)(2,1)} %get-tuple-element.34), kind=kLoop, calls=%fused_computation.27 | loop fusion | flops 75497472 | bytes 75497472 | tf_op jit(solution)/shard_map/concatenate | solution.py:141
  645.6 54.6 %fusion.23 = f32[1024,12288]{1,0:T(8,128)} fusion(f32[1024,12288]{1,0:T(8,128)} %fusion.77, bf16[1536,1024]{1,0:T(8,128)(2,1)S(1)} %collective-permute-done.2, bf16[1536,6144]{1,0:T(8,128)(2,1)} %collective-permute-done.4, bf16[1536,6144]{1,0:T(8,128)(2,1)} %collective-permute-done.3), kind=kOutput, calls=%fused_computation.41 | convolution fusion | flops 38742786048 | bytes 141557760 | tf_op jit(solution)/shard_map/dot_general | solution.py:59
  700.1 92.9 %fusion.40 = (f32[2048]{0:T(1024)}, f32[1536]{0:T(1024)S(1)}, f32[1536,2048]{1,0:T(8,128)}) fusion(bf16[1536,2048]{1,0:T(8,128)(2,1)} %copy-done.1, f32[1536]{0:T(1024)S(1)} %copy-done.19, f32[2048]{0:T(1024)S(1)} %copy-done.16, bf16[1536,12288]{1,0:T(8,128)(2,1)} %pad_maximum_fusion, bf16[2048,12288]{1,0:T(8,128)(2,1)} %all-gather.9.cloned.1.call-done), kind=kOutput, calls=%fused_computation.58 | convolution fusion | flops 77331431424 | bytes 106983424 | tf_op jit(solution)/shard_map/dot_general | solution.py:147
  793.1 13.7 fusion.76
  823.2 19.1 %convolution_convert_fusion.1 = bf16[1536,2048]{1,0:T(8,128)(2,1)} fusion(bf16[1536,2048]{1,0:T(8,128)(2,1)} %fusion.76, bf16[2048,2048]{1,0:T(8,128)(2,1)} %all-gather.7.cloned.1.call-done), kind=kOutput, calls=%fused_computation.83 | convolution fusion | flops 12888047616 | bytes 20971520 | tf_op jit(solution)/shard_map/dot_general | solution.py:155
  874.1 22.3 %fusion.84 = f32[3,4,512,512,4]{3,2,4,1,0:T(8,128)} fusion(bf16[3,512,4,128,1]{1,3,4,2,0:T(8,128)(2,1)S(1)} %bitcast.217, bf16[3,512,4,4,128]{1,4,3,2,0:T(8,128)(2,1)} %copy.115), kind=kOutput, calls=%fused_computation.204 | convolution fusion | flops 3221225472 | bytes 58195968 | tf_op jit(solution)/shard_map/bqkgd,bskd->bkgqs/dot_general | solution.py:44
  896.4 67.8 %fusion.28 = f32[3,4,128,4,512]{4,2,3,1,0:T(8,128)} fusion(f32[3,4,512,512,4]{3,2,4,1,0:T(8,128)} %fusion.84, bf16[3,512,4,64]{3,1,2,0:T(8,128)(2,1)S(1)} %copy-done.13, bf16[3,512,4,64]{3,1,2,0:T(8,128)(2,1)} %copy.94, f32[3,4,4,512,512]{3,4,2,1,0:T(8,128)} %get-tuple-element.120, f32[3,4,4,512]{3,2,1,0:T(4,128)S(1)} %copy-done.34), kind=kOutput, calls=%fused_computation.44 | convolution fusion | flops 3312476672 | bytes 114917376 | tf_op jit(solution)/shard_map/bkgqs,bskd->bqkgd/dot_general | solution.py:48
  1004.4 12.7 copy.108
  1017.1 66.9 %fusion.65 = f32[3,512,4,128]{1,3,2,0:T(8,128)} fusion(f32[3,4,512,512,4]{3,2,4,1,0:T(8,128)} %fusion.84, bf16[3,512,4,4,64]{4,1,3,2,0:T(8,128)(2,1)} %bitcast.222, bf16[3,512,4,4,64]{4,1,3,2,0:T(8,128)(2,1)} %copy.99, f32[3,4,4,512,512]{3,4,2,1,0:T(8,128)} %get-tuple-element.120, f32[3,4,4,512]{3,2,1,0:T(4,128)S(1)} %copy-done.35), kind=kOutput, calls=%fused_computation.101 | convolution fusion | flops 3321913856 | bytes 110198784 | tf_op jit(solution)/shard_map/bkgqs,bqkgd->bskd/dot_general | solution.py:49
  1093.8 20.9 %fusion.62 = f32[3,512,4,128]{1,3,2,0:T(8,128)} fusion(bf16[3,512,4,4,128]{1,4,3,2,0:T(8,128)(2,1)} %copy.115, f32[3,4,4,512,512]{3,4,2,1,0:T(8,128)} %get-tuple-element.120, f32[3,4,4,512]{3,2,1,0:T(4,128)S(1)} %copy-done.36), kind=kOutput, calls=%fused_computation.100 | convolution fusion | flops 3246391296 | bytes 59867136 | tf_op jit(solution)/shard_map/bkgqs,bqkgd->bskd/dot_general | solution.py:45
  1119.8 15.5 bitcast_dynamic-update-slice_fusion
  1140.4 15.3 fusion.78
  1174.8 15.8 convolution_add_fusion.2
  1191.5 29.7 %fusion.53 = (f32[2048]{0:T(1024)S(1)}, f32[1536]{0:T(1024)S(1)}, f32[1536,2048]{1,0:T(8,128)}) fusion(bf16[3,512,2048]{2,1,0:T(8,128)(2,1)} %param.10, f32[1536]{0:T(1024)S(1)} %copy-done.24, f32[2048]{0:T(1024)S(1)} %copy-done.22, bf16[1536,3072]{1,0:T(8,128)(2,1)} %copy-done.8, bf16[2048,3072]{1,0:T(8,128)(2,1)} %all-gather.5.cloned.1.call-done), kind=kOutput, calls=%fused_computation.78 | convolution fusion | flops 19349368832 | bytes 40923136 | tf_op jit(solution)/shard_map/dot_general | solution.py:173
  1221.2 33.4 %all-reduce.3 = (f32[2048]{0:T(1024)S(1)}, f32[3072]{0:T(1024)S(1)}, f32[2048]{0:T(1024)S(1)}) all-reduce(f32[2048]{0:T(1024)S(1)} %get-tuple-element.29, f32[3072]{0:T(1024)S(1)} %get-tuple-element.36, f32[2048]{0:T(1024)S(1)} %copy-done.30), channel_id=2, replica_groups=mesh['fsdp'=16] {'fsdp'}, use_global_device_ids=true, to_apply=%region_8.9.clone | all-reduce | flops 7168 | bytes 57344
  1256.4 20.2 %fusion.48 = bf16[1536,2048]{1,0:T(8,128)(2,1)} fusion(bf16[3,512,2048]{2,1,0:T(8,128)(2,1)} %param.10, f32[1536,2048]{1,0:T(8,128)} %get-tuple-element.124, f32[1536]{0:T(1024)S(1)} %broadcast_multiply_fusion, f32[2048]{0:T(1024)S(1)} %copy-done.22, f32[1536]{0:T(1024)S(1)} %copy-done.24, f32[1536]{0:T(1024)S(1)} %copy-done.26, ...), kind=kLoop, calls=%fused_computation.73 | loop fusion | flops 56623104 | bytes 50372608 | tf_op jit(solution)/shard_map/convert_element_type | solution.py:176
  1276.6 49.8 %fusion.38 = bf16[1536,2048]{1,0:T(8,128)(2,1)} fusion(bf16[1536,2048]{1,0:T(8,128)(2,1)} %copy-done.1, bf16[1536,6144]{1,0:T(8,128)(2,1)} %copy-done, bf16[6144,2048]{1,0:T(8,128)(2,1)} %all-gather.11.cloned.1.call-done), kind=kOutput, calls=%fused_computation.56 | convolution fusion | flops 38664142848 | bytes 56623104 | tf_op jit(solution)/shard_map/dot_general | solution.py:177
  1326.4 327.3 %reduce-scatter.9.cloned.1.call-done = f32[128,12288]{1,0:T(8,128)} async-done(((f32[1024,12288]{1,0:T(8,128)}), f32[128,12288]{1,0:T(8,128)}) %reduce-scatter.9.cloned.1.call-update) | async-done | bytes 6291472 | tf_op jit(solution)/shard_map/reduce_scatter | solution.py:78
  (218 shorter events, 279.3 us)
Async XLA Ops:
  7.2 23.7 %copy-start.31 = (s32[3,512]{1,0:T(4,128)S(1)}, s32[3,512]{1,0:T(4,128)}, u32[]{:S(2)}) copy-start(s32[3,512]{1,0:T(4,128)} %param.11) | copy-start | bytes 18436
  7.2 68.2 %all-gather.5.cloned.1.call-start = ((), (), s32[]{:S(2)}) async-start(), calls=%async_computation.4 | async-start | bytes 13369344 | tf_op jit(solution)/shard_map/all_gather | solution.py:81
  7.9 247.0 %all-gather.7.cloned.1.call-start = ((), (), s32[]{:S(2)}) async-start(), calls=%async_computation.5 | async-start | bytes 8912896 | tf_op jit(solution)/shard_map/all_gather | solution.py:81
  8.7 306.1 %all-gather.9.cloned.1.call-start = ((), (), s32[]{:S(2)}) async-start(), calls=%async_computation.6 | async-start | bytes 53477376 | tf_op jit(solution)/shard_map/all_gather | solution.py:81
  9.4 482.9 %all-gather.11.cloned.1.call-start = ((), (), s32[]{:S(2)}) async-start(), calls=%async_computation.7 | async-start | bytes 26738688 | tf_op jit(solution)/shard_map/all_gather | solution.py:81
  10.0 1316.4 %reduce-scatter.7.cloned.1.call-start = ((), (), s32[]{:S(2)}) async-start(), calls=%async_computation.9 | async-start | bytes 9437184 | tf_op jit(solution)/shard_map/reduce_scatter | solution.py:78
  39.3 132.5 %copy-start.9 = (f32[3,512,32]{1,2,0:T(8,128)}, f32[3,512,32]{1,2,0:T(8,128)S(1)}, u32[]{:S(2)}) copy-start(f32[3,512,32]{1,2,0:T(8,128)S(1)} %get-tuple-element.118) | copy-start | bytes 589828
  184.2 28.2 %copy-start.6 = (bf16[3,512,512]{1,2,0:T(8,128)(2,1)S(1)}, bf16[3,512,512]{1,2,0:T(8,128)(2,1)}, u32[]{:S(2)}) copy-start(bf16[3,512,512]{1,2,0:T(8,128)(2,1)} %copy.90) | copy-start | bytes 4718596
  212.4 20.1 %copy-start.33 = (f32[3,4,4,512]{3,2,1,0:T(4,128)}, f32[3,4,4,512]{3,2,1,0:T(4,128)S(1)}, u32[]{:S(2)}) copy-start(f32[3,4,4,512]{3,2,1,0:T(4,128)S(1)} %get-tuple-element.119) | copy-start | bytes 294916
  254.9 21.4 %copy-start.15 = (f32[2048]{0:T(1024)S(1)}, f32[2048]{0:T(1024)}, u32[]{:S(2)}) copy-start(f32[2048]{0:T(1024)} %get-tuple-element.114) | copy-start | bytes 24580
  433.9 27.9 %collective-permute-start = (bf16[1536,3072]{1,0:T(8,128)(2,1)S(1)}, bf16[1536,3072]{1,0:T(8,128)(2,1)}, u32[]{:S(2)}, u32[]{:S(2)}) collective-permute-start(bf16[1536,3072]{1,0:T(8,128)(2,1)S(1)} %get-tuple-element.38), channel_id=1, source_target_pairs={{0,1},{1,0},{2,3},{3,2},{4,5},{5,4},{6,7},{7,6},{8,9},{9,8},{10,11... | collective-permute-start | bytes 28311560 | tf_op jit(solution)/shard_map/ppermute | solution.py:75
  434.2 25.0 %collective-permute-start.1 = (bf16[1536,2048]{1,0:T(8,128)(2,1)S(1)}, bf16[1536,2048]{1,0:T(8,128)(2,1)S(1)}, u32[]{:S(2)}, u32[]{:S(2)}) collective-permute-start(bf16[1536,2048]{1,0:T(8,128)(2,1)S(1)} %bitcast.208), channel_id=1, source_target_pairs={{0,1},{1,0},{2,3},{3,2},{4,5},{5,4},{6,7},{7,6},{8,9},{9,8},{10,11... | collective-permute-start | bytes 18874376 | tf_op jit(solution)/shard_map/ppermute | solution.py:75
  557.3 88.2 %collective-permute-start.4 = (bf16[1536,6144]{1,0:T(8,128)(2,1)}, bf16[1536,6144]{1,0:T(8,128)(2,1)}, u32[]{:S(2)}, u32[]{:S(2)}) collective-permute-start(bf16[1536,6144]{1,0:T(8,128)(2,1)} %get-tuple-element.35), channel_id=1, source_target_pairs={{0,1},{1,0},{2,3},{3,2},{4,5},{5,4},{6,7},{7,6},{8,9},{9,8},{10,11... | collective-permute-start | bytes 56623112 | tf_op jit(solution)/shard_map/ppermute | solution.py:75
  557.6 88.0 %collective-permute-start.3 = (bf16[1536,6144]{1,0:T(8,128)(2,1)}, bf16[1536,6144]{1,0:T(8,128)(2,1)}, u32[]{:S(2)}, u32[]{:S(2)}) collective-permute-start(bf16[1536,6144]{1,0:T(8,128)(2,1)} %get-tuple-element.34), channel_id=1, source_target_pairs={{0,1},{1,0},{2,3},{3,2},{4,5},{5,4},{6,7},{7,6},{8,9},{9,8},{10,11... | collective-permute-start | bytes 56623112 | tf_op jit(solution)/shard_map/ppermute | solution.py:75
  571.2 74.4 %collective-permute-start.2 = (bf16[1536,1024]{1,0:T(8,128)(2,1)}, bf16[1536,1024]{1,0:T(8,128)(2,1)S(1)}, u32[]{:S(2)}, u32[]{:S(2)}) collective-permute-start(bf16[1536,1024]{1,0:T(8,128)(2,1)} %get-tuple-element.92), channel_id=1, source_target_pairs={{0,1},{1,0},{2,3},{3,2},{4,5},{5,4},{6,7},{7,6},{8,9},{9,8},{10,11... | collective-permute-start | bytes 9437192 | tf_op jit(solution)/shard_map/ppermute | solution.py:75
  645.5 54.6 %copy-start.16 = (f32[2048]{0:T(1024)S(1)}, f32[2048]{0:T(1024)}, u32[]{:S(2)}) copy-start(f32[2048]{0:T(1024)} %get-tuple-element.114) | copy-start | bytes 24580
  645.5 54.6 %copy-start.19 = (f32[1536]{0:T(1024)S(1)}, f32[1536]{0:T(1024)}, u32[]{:S(2)}) copy-start(f32[1536]{0:T(1024)} %copy-done.18) | copy-start | bytes 18436
  806.7 35.6 %collective-permute-start.6 = (bf16[1536,2048]{1,0:T(8,128)(2,1)}, bf16[1536,2048]{1,0:T(8,128)(2,1)S(1)}, u32[]{:S(2)}, u32[]{:S(2)}) collective-permute-start(bf16[1536,2048]{1,0:T(8,128)(2,1)} %fusion.76), channel_id=1, source_target_pairs={{0,1},{1,0},{2,3},{3,2},{4,5},{5,4},{6,7},{7,6},{8,9},{9,8},{10,11... | collective-permute-start | bytes 18874376 | tf_op jit(solution)/shard_map/ppermute | solution.py:75
  813.7 28.6 %collective-permute-start.5 = (bf16[1536,1024]{1,0:T(8,128)(2,1)}, bf16[1536,1024]{1,0:T(8,128)(2,1)S(1)}, u32[]{:S(2)}, u32[]{:S(2)}) collective-permute-start(bf16[1536,1024]{1,0:T(8,128)(2,1)} %get-tuple-element.76), channel_id=1, source_target_pairs={{0,1},{1,0},{2,3},{3,2},{4,5},{5,4},{6,7},{7,6},{8,9},{9,8},{10,11... | collective-permute-start | bytes 9437192 | tf_op jit(solution)/shard_map/ppermute | solution.py:75
  851.8 474.6 %reduce-scatter.11.cloned.1.call-start = ((), (), s32[]{:S(2)}) async-start(), calls=%async_computation.11 | async-start | bytes 28311552 | tf_op jit(solution)/shard_map/reduce_scatter | solution.py:78
  852.4 474.0 %reduce-scatter.5.cloned.1.call-start = ((), (), s32[]{:S(2)}) async-start(), calls=%async_computation.8 | async-start | bytes 14155776 | tf_op jit(solution)/shard_map/reduce_scatter | solution.py:78
  874.1 22.3 %copy-start.13 = (bf16[3,512,4,64]{3,1,2,0:T(8,128)(2,1)S(1)}, bf16[3,512,4,64]{3,1,2,0:T(8,128)(2,1)}, u32[]{:S(2)}) copy-start(bf16[3,512,4,64]{3,1,2,0:T(8,128)(2,1)} %copy.141) | copy-start | bytes 2359300
  874.1 22.3 %copy-start.34 = (f32[3,4,4,512]{3,2,1,0:T(4,128)S(1)}, f32[3,4,4,512]{3,2,1,0:T(4,128)}, u32[]{:S(2)}) copy-start(f32[3,4,4,512]{3,2,1,0:T(4,128)} %copy-done.33) | copy-start | bytes 294916
  1138.3 17.7 %slice-start = ((s8[6291456]{0:T(1024)(128)(4,1)}), s8[4194304]{0:T(1024)(128)(4,1)S(1)}, s32[]{:S(2)}) async-start(s8[6291456]{0:T(1024)(128)(4,1)} %bitcast.200), calls=%async_computation.12 | async-start | bytes 8388608
  1140.4 15.7 slice-start.1
  1155.6 19.2 %collective-permute-start.8 = (bf16[1536,3072]{1,0:T(8,128)(2,1)S(1)}, bf16[1536,3072]{1,0:T(8,128)(2,1)}, u32[]{:S(2)}, u32[]{:S(2)}) collective-permute-start(bf16[1536,3072]{1,0:T(8,128)(2,1)S(1)} %get-tuple-element.22), channel_id=1, source_target_pairs={{0,1},{1,0},{2,3},{3,2},{4,5},{5,4},{6,7},{7,6},{8,9},{9,8},{10,11... | collective-permute-start | bytes 28311560 | tf_op jit(solution)/shard_map/ppermute | solution.py:75
  1159.3 15.6 collective-permute-start.7
  1190.7 463.0 %reduce-scatter.9.cloned.1.call-start = ((), (), s32[]{:S(2)}) async-start(), calls=%async_computation.10 | async-start | bytes 56623104 | tf_op jit(solution)/shard_map/reduce_scatter | solution.py:78
  1191.5 29.7 %copy-start.30 = (f32[2048]{0:T(1024)S(1)}, f32[2048]{0:T(1024)}, u32[]{:S(2)}) copy-start(f32[2048]{0:T(1024)} %get-tuple-element.27) | copy-start | bytes 24580
  1191.5 65.0 %copy-start.17 = (f32[2048]{0:T(1024)S(1)}, f32[2048]{0:T(1024)}, u32[]{:S(2)}) copy-start(f32[2048]{0:T(1024)} %get-tuple-element.114) | copy-start | bytes 24580
  1191.5 64.9 %copy-start.20 = (f32[1536]{0:T(1024)S(1)}, f32[1536]{0:T(1024)}, u32[]{:S(2)}) copy-start(f32[1536]{0:T(1024)} %copy-done.18) | copy-start | bytes 18436
  1191.5 64.9 %copy-start.26 = (f32[1536]{0:T(1024)S(1)}, f32[1536]{0:T(1024)}, u32[]{:S(2)}) copy-start(f32[1536]{0:T(1024)} %copy-done.25) | copy-start | bytes 18436
  (26 other events, 167.6 us)
Sparse Core Ops, SparseCore 0:
  10.2 65.1 all-gather.4
  77.7 48.6 all-gather.6
  128.6 186.1 all-gather.8
  316.8 103.3 all-gather.10
  851.9 164.8 reduce-scatter.6
  1021.5 181.0 reduce-scatter.10
  1207.3 103.5 reduce-scatter.4
  1315.7 337.9 reduce-scatter.8
